TPU v7x, 32 devices: a whole 2x2x4 slice. The times are simulated.
32 devices in a mesh: grid: 2 (over x), prow: 4 (over y, core), pcol: 4 (over z).
Axes of the slice: x: 2, y: 2, z: 4, core: 2. Of those that a mesh axis runs over, the one named last changes fastest.
Arguments:
- sub_rhs: float32 [2, 3, 64, 3072], P('grid', None, None, 'prow'), may hold values from -6 to 6
- root_rhs: float32 [64, 3072], P(None, 'prow'), may hold values from -6 to 6
- diag_inverse: bfloat16 [3, 3072, 6144], P(None, 'prow', ('grid', 'pcol'))
- root_inverse: bfloat16 [3072, 3072], P('prow', 'grid')
- inner_factor: bfloat16 [3, 6144, 3072], P(None, ('grid', 'pcol'), 'prow'), may hold values from -0.078125 to 0.078125
- inner_mask: int32 [3, 48, 24], P(None, ('grid', 'pcol')), may hold values 0 or 1
- root_factor: bfloat16 [3, 6144, 3072], P(None, ('grid', 'pcol'), 'prow'), may hold values from -0.078125 to 0.078125
- root_mask: int32 [3, 48, 24], P(None, ('grid', 'pcol')), may hold values 0 or 1
Outputs:
- sub_solution: float32 [3, 64, 6144], P(None, None, ('grid', 'pcol'))
- root_solution: float32 [64, 3072], P(None, 'grid')
Inputs may be any that keep to these rules, and one draw needn't show every extreme that they name: `inner_mask`: 1 keeps a tile of 128 x 128 entries, 0 makes it zero. `root_mask`: 1 keeps a tile of 128 x 128 entries, 0 makes it zero.
All inputs are finite; a program needn't handle non-finite values. No bound on the sum of `inner_mask` or of `root_mask` on one device may be relied on, other than what follows from the above.
Results may differ from a plain program's by a relative error of at most 0.0065.
Values sent between devices are 32-bit elements; how exact they have to be, the bound alone decides.
A program may use at most 64 MiB of HBM per device.

v0:
```python
import jax
import jax.numpy as jnp
from jax import lax
from jax.sharding import PartitionSpec as P

NS = 3072
LEVELS = 3
TILE = 128


def from_partner(shard, axis, bit):
    return lax.ppermute(shard, axis, [(i, i ^ 1 << bit) for i in range(lax.axis_size(axis))])


def selector(positions, count):
    return (positions[:, None] // TILE == jnp.arange(count)[None, :]).astype(jnp.float32)


def masked(factor, mask, row_select, col_select):
    expanded = jnp.dot(jnp.dot(row_select, mask.astype(jnp.float32)), col_select.T)
    return factor * expanded.astype(jnp.bfloat16)


def solve_block(residual, inverse):
    partial_sum = jnp.dot(
        residual.astype(jnp.bfloat16), inverse, preferred_element_type=jnp.float32
    )
    return lax.psum(partial_sum, "prow")


def group_sum(partial_sum, owners):
    summed = partial_sum
    for bit_number in range(owners.bit_length() - 1):
        summed = summed + from_partner(summed, "pcol", bit_number)
    return summed


def shards(
    sub_rhs, root_rhs, diag_inverse, root_inverse, inner_factor, inner_mask, root_factor, root_mask
):
    rows_here = inner_factor.shape[1]
    out_cols = inner_factor.shape[2]
    owners = NS // rows_here
    own_tree = lax.axis_index("pcol") // owners
    col_positions = lax.axis_index("prow") * out_cols + jnp.arange(out_cols)
    row_select = selector(jnp.arange(rows_here), inner_mask.shape[1])
    col_select = selector(col_positions, inner_mask.shape[2])
    own_rhs = lax.dynamic_index_in_dim(sub_rhs, own_tree, 0, keepdims=False)
    kept = []
    solved_all = []
    pair = 0
    for level in range(LEVELS):
        residual = own_rhs[level]
        if level > 0:
            local_update = jnp.zeros(residual.shape, jnp.float32)
            for source in range(level):
                factor_tile = masked(inner_factor[pair], inner_mask[pair], row_select, col_select)
                local_update = local_update + jnp.dot(
                    kept[source], factor_tile, preferred_element_type=jnp.float32
                )
                pair += 1
            residual = residual - group_sum(local_update, owners)
        solved = solve_block(residual, diag_inverse[level])
        solved_all.append(solved)
        kept.append(solved.astype(jnp.bfloat16))
    root_local = jnp.zeros(root_rhs.shape, jnp.float32)
    for source in range(LEVELS):
        factor_tile = masked(root_factor[source], root_mask[source], row_select, col_select)
        root_local = root_local + jnp.dot(
            kept[source], factor_tile, preferred_element_type=jnp.float32
        )
    across = lax.psum(root_local, "pcol")
    root_update = lax.psum(across, "grid")
    root_solution = solve_block(root_rhs - root_update, root_inverse)
    return (jnp.stack(solved_all), root_solution)


def solution(mesh):
    return jax.shard_map(
        shards,
        mesh=mesh,
        in_specs=(
            P("grid", None, None, "prow"),
            P(None, "prow"),
            P(None, "prow", ("grid", "pcol")),
            P("prow", "grid"),
            P(None, ("grid", "pcol"), "prow"),
            P(None, ("grid", "pcol"), None),
            P(None, ("grid", "pcol"), "prow"),
            P(None, ("grid", "pcol"), None),
        ),
        out_specs=(P(None, None, ("grid", "pcol")), P(None, "grid")),
        check_vma=False,
    )
```

profile of v0, /device:TPU:0, one launch (start us, length us, event | category | flops | bytes accessed | tf_op | source)
XLA Modules:
  0.0 262.5 jit_solution(7148002226130458398)
XLA Ops:
  7.2 2.5 fusion.22
  11.0 34.6 %all-reduce.7.cloned.1.call-done = f32[64,768]{1,0:T(8,128)} async-done(((f32[64,768]{1,0:T(8,128)}), f32[64,768]{1,0:T(8,128)}) %all-reduce.7.cloned.1.call-update) | async-done | bytes 196624 | tf_op jit(solution)/shard_map/psum | solution.py:28
  45.7 2.1 fusion.11
  50.3 3.2 %collective-permute-done = f32[64,768]{1,0:T(8,128)S(1)} collective-permute-done((f32[64,768]{1,0:T(8,128)S(1)}, f32[64,768]{1,0:T(8,128)S(1)}, u32[]{:S(2)}, u32[]{:S(2)}) %collective-permute-start) | collective-permute-done | bytes 196640 | tf_op jit(solution)/shard_map/ppermute | solution.py:12
  53.6 2.5 collective-permute-start.1
  56.0 1.7 fusion.37
  57.7 5.2 %collective-permute-done.1 = f32[64,768]{1,0:T(8,128)S(1)} collective-permute-done((f32[64,768]{1,0:T(8,128)S(1)}, f32[64,768]{1,0:T(8,128)S(1)}, u32[]{:S(2)}, u32[]{:S(2)}) %collective-permute-start.1) | collective-permute-done | bytes 196640 | tf_op jit(solution)/shard_map/ppermute | solution.py:12
  62.9 2.3 fusion.19
  66.3 32.6 %all-reduce.9.cloned.1.call-done = f32[64,768]{1,0:T(8,128)} async-done(((f32[64,768]{1,0:T(8,128)}), f32[64,768]{1,0:T(8,128)}) %all-reduce.9.cloned.1.call-update) | async-done | bytes 196624 | tf_op jit(solution)/shard_map/psum | solution.py:28
  98.8 2.8 %fusion.9 = f32[64,768]{1,0:T(8,128)} fusion(bf16[768,24]{1,0:T(8,128)(2,1)S(1)} %fusion.39, bf16[3,768,768]{2,1,0:T(8,128)(2,1)} %param.12, s32[768]{0:T(1024)S(1)} %copy-done.10, f32[64,768]{1,0:T(8,128)} %all-reduce.9.cloned.1.call-done), kind=kOutput, calls=%fused_computation.15 | convolution fusion | flops 104466432 | bytes 1612800 | tf_op jit(solution)/shard_map/dot_general | solution.py:58
  101.7 2.2 fusion.33
  106.4 3.2 %collective-permute-done.2 = f32[64,768]{1,0:T(8,128)S(1)} collective-permute-done((f32[64,768]{1,0:T(8,128)S(1)}, f32[64,768]{1,0:T(8,128)S(1)}, u32[]{:S(2)}, u32[]{:S(2)}) %collective-permute-start.2) | collective-permute-done | bytes 196640 | tf_op jit(solution)/shard_map/ppermute | solution.py:12
  110.6 2.5 collective-permute-start.3
  113.0 2.8 %fusion.7 = f32[64,768]{1,0:T(8,128)} fusion(bf16[768,24]{1,0:T(8,128)(2,1)} %fusion.37, bf16[3,768,768]{2,1,0:T(8,128)(2,1)} %param.14, s32[768]{0:T(1024)} %add_select_fusion, f32[64,768]{1,0:T(8,128)S(1)} %copy-done.4), kind=kOutput, calls=%fused_computation.13 | convolution fusion | flops 104466432 | bytes 1773568 | tf_op jit(solution)/shard_map/dot_general | solution.py:69
  115.9 4.1 %collective-permute-done.3 = f32[64,768]{1,0:T(8,128)} collective-permute-done((f32[64,768]{1,0:T(8,128)S(1)}, f32[64,768]{1,0:T(8,128)}, u32[]{:S(2)}, u32[]{:S(2)}) %collective-permute-start.3) | collective-permute-done | bytes 196640 | tf_op jit(solution)/shard_map/ppermute | solution.py:12
  120.0 2.4 fusion.15
  122.5 2.1 fusion.34
  124.6 31.4 %all-reduce.11.cloned.1.call-done = f32[64,768]{1,0:T(8,128)} async-done(((f32[64,768]{1,0:T(8,128)}), f32[64,768]{1,0:T(8,128)}) %all-reduce.11.cloned.1.call-update) | async-done | bytes 196624 | tf_op jit(solution)/shard_map/psum | solution.py:28
  156.0 2.8 %fusion.35 = f32[64,768]{1,0:T(8,128)} fusion(f32[64,768]{1,0:T(8,128)S(1)} %fusion.34, bf16[768,24]{1,0:T(8,128)(2,1)S(1)} %copy-done.6, bf16[3,768,768]{2,1,0:T(8,128)(2,1)} %param.14, s32[768]{0:T(1024)S(1)} %copy-done.11, f32[64,768]{1,0:T(8,128)} %all-reduce.11.cloned.1.call-done), kind=kOutput, calls=%fused_computation.41 | convolution fusion | flops 104515584 | bytes 1809408 | tf_op jit(solution)/shard_map/dot_general | solution.py:69
  158.9 35.1 %all-reduce.13.cloned.1.call-done = f32[64,768]{1,0:T(8,128)} async-done(((f32[64,768]{1,0:T(8,128)}), f32[64,768]{1,0:T(8,128)}) %all-reduce.13.cloned.1.call-update) | async-done | bytes 196624 | tf_op jit(solution)/shard_map/psum | solution.py:72
  194.1 24.1 %all-reduce.15.cloned.1.call-done = f32[64,768]{1,0:T(8,128)} async-done(((f32[64,768]{1,0:T(8,128)}), f32[64,768]{1,0:T(8,128)}) %all-reduce.15.cloned.1.call-update) | async-done | bytes 196624 | tf_op jit(solution)/shard_map/psum | solution.py:73
  218.3 2.2 fusion.62
  221.4 32.5 %all-reduce.17.cloned.1.call-done = f32[64,1536]{1,0:T(8,128)} async-done(((f32[64,1536]{1,0:T(8,128)}), f32[64,1536]{1,0:T(8,128)}) %all-reduce.17.cloned.1.call-update) | async-done | bytes 393232 | tf_op jit(solution)/shard_map/psum | solution.py:28
  253.9 1.8 copy.16
  (48 shorter events, 9.4 us)
Async XLA Ops:
  7.2 211.1 %copy-start = (bf16[768,1536]{1,0:T(8,128)(2,1)S(1)}, bf16[768,1536]{1,0:T(8,128)(2,1)}, u32[]{:S(2)}) copy-start(bf16[768,1536]{1,0:T(8,128)(2,1)} %param.11) | copy-start | bytes 7077892
  7.2 2.7 %copy-start.8 = (s32[3,6,24]{2,1,0:T(8,128)S(1)}, s32[3,6,24]{2,1,0:T(8,128)}, u32[]{:S(2)}) copy-start(s32[3,6,24]{2,1,0:T(8,128)} %param.13) | copy-start | bytes 5188
  7.2 38.5 %all-reduce.7.cloned.1.call-start = ((), (), s32[]{:S(2)}) async-start(), calls=%async_computation | async-start | bytes 393216 | tf_op jit(solution)/shard_map/psum | solution.py:28
  9.8 89.0 %all-reduce.9.cloned.1.call-start = ((), (), s32[]{:S(2)}) async-start(), calls=%async_computation.1 | async-start | bytes 393216 | tf_op jit(solution)/shard_map/psum | solution.py:28
  11.0 51.9 %copy-start.1 = (f32[1,3,64,768]{3,2,1,0:T(8,128)S(1)}, f32[1,3,64,768]{3,2,1,0:T(8,128)}, u32[]{:S(2)}) copy-start(f32[1,3,64,768]{3,2,1,0:T(8,128)} %param.8) | copy-start | bytes 1769476
  47.8 5.7 %collective-permute-start = (f32[64,768]{1,0:T(8,128)S(1)}, f32[64,768]{1,0:T(8,128)S(1)}, u32[]{:S(2)}, u32[]{:S(2)}) collective-permute-start(f32[64,768]{1,0:T(8,128)S(1)} %fusion.11), channel_id=1, source_target_pairs={{0,1},{1,0},{2,3},{3,2},{4,5},{5,4},{6,7},{7,6},{8,9},{9,8},{10,11... | collective-permute-start | bytes 589832 | tf_op jit(solution)/shard_map/ppermute | solution.py:12
  53.6 11.7 %copy-start.9 = (s32[3,6,24]{2,1,0:T(8,128)S(1)}, s32[3,6,24]{2,1,0:T(8,128)}, u32[]{:S(2)}) copy-start(s32[3,6,24]{2,1,0:T(8,128)} %param.15) | copy-start | bytes 5188
  53.6 9.4 %collective-permute-start.1 = (f32[64,768]{1,0:T(8,128)S(1)}, f32[64,768]{1,0:T(8,128)S(1)}, u32[]{:S(2)}, u32[]{:S(2)}) collective-permute-start(f32[64,768]{1,0:T(8,128)S(1)} %add.60), channel_id=1, source_target_pairs={{0,2},{1,3},{2,0},{3,1},{4,6},{5,7},{6,4},{7,5},{8,10},{9,11},{10,... | collective-permute-start | bytes 589832 | tf_op jit(solution)/shard_map/ppermute | solution.py:12
  57.7 41.1 %copy-start.10 = (s32[768]{0:T(1024)S(1)}, s32[768]{0:T(1024)}, u32[]{:S(2)}) copy-start(s32[768]{0:T(1024)} %add_select_fusion) | copy-start | bytes 9220
  65.2 36.4 %copy-start.3 = (f32[64,768]{1,0:T(8,128)S(1)}, f32[64,768]{1,0:T(8,128)}, u32[]{:S(2)}) copy-start(f32[64,768]{1,0:T(8,128)} %all-reduce.7.cloned.1.call-done) | copy-start | bytes 589828
  65.2 90.8 %all-reduce.11.cloned.1.call-start = ((), (), s32[]{:S(2)}) async-start(), calls=%async_computation.2 | async-start | bytes 393216 | tf_op jit(solution)/shard_map/psum | solution.py:28
  101.7 11.4 %copy-start.4 = (f32[64,768]{1,0:T(8,128)S(1)}, f32[64,768]{1,0:T(8,128)}, u32[]{:S(2)}) copy-start(f32[64,768]{1,0:T(8,128)} %all-reduce.9.cloned.1.call-done) | copy-start | bytes 589828
  103.9 2.5 copy-start.7
  103.9 5.7 %collective-permute-start.2 = (f32[64,768]{1,0:T(8,128)S(1)}, f32[64,768]{1,0:T(8,128)S(1)}, u32[]{:S(2)}, u32[]{:S(2)}) collective-permute-start(f32[64,768]{1,0:T(8,128)S(1)} %fusion.33), channel_id=1, source_target_pairs={{0,1},{1,0},{2,3},{3,2},{4,5},{5,4},{6,7},{7,6},{8,9},{9,8},{10,11... | collective-permute-start | bytes 589832 | tf_op jit(solution)/shard_map/ppermute | solution.py:12
  110.6 9.5 %collective-permute-start.3 = (f32[64,768]{1,0:T(8,128)S(1)}, f32[64,768]{1,0:T(8,128)}, u32[]{:S(2)}, u32[]{:S(2)}) collective-permute-start(f32[64,768]{1,0:T(8,128)S(1)} %add.63), channel_id=1, source_target_pairs={{0,2},{1,3},{2,0},{3,1},{4,6},{5,7},{6,4},{7,5},{8,10},{9,11},{10,... | collective-permute-start | bytes 589832 | tf_op jit(solution)/shard_map/ppermute | solution.py:12
  115.9 6.6 %copy-start.11 = (s32[768]{0:T(1024)S(1)}, s32[768]{0:T(1024)}, u32[]{:S(2)}) copy-start(s32[768]{0:T(1024)} %add_select_fusion) | copy-start | bytes 9220
  122.4 33.6 %copy-start.6 = (bf16[768,24]{1,0:T(8,128)(2,1)S(1)}, bf16[768,24]{1,0:T(8,128)(2,1)}, u32[]{:S(2)}) copy-start(bf16[768,24]{1,0:T(8,128)(2,1)} %fusion.36) | copy-start | bytes 110596
  122.4 71.6 %all-reduce.13.cloned.1.call-start = ((), (), s32[]{:S(2)}) async-start(), calls=%async_computation.3 | async-start | bytes 393216 | tf_op jit(solution)/shard_map/psum | solution.py:72
  124.6 93.6 %copy-start.2 = (f32[64,768]{1,0:T(8,128)S(1)}, f32[64,768]{1,0:T(8,128)}, u32[]{:S(2)}) copy-start(f32[64,768]{1,0:T(8,128)} %param.9) | copy-start | bytes 589828
  158.9 59.4 %all-reduce.15.cloned.1.call-start = ((), (), s32[]{:S(2)}) async-start(), calls=%async_computation.4 | async-start | bytes 393216 | tf_op jit(solution)/shard_map/psum | solution.py:73
  194.1 26.4 %copy-start.5 = (f32[64,768]{1,0:T(8,128)S(1)}, f32[64,768]{1,0:T(8,128)}, u32[]{:S(2)}) copy-start(f32[64,768]{1,0:T(8,128)} %all-reduce.11.cloned.1.call-done) | copy-start | bytes 589828
  194.1 59.8 %all-reduce.17.cloned.1.call-start = ((), (), s32[]{:S(2)}) async-start(), calls=%async_computation.5 | async-start | bytes 786432 | tf_op jit(solution)/shard_map/psum | solution.py:28
Sparse Core Ops, SparseCore 0:
  10.9 34.7 all-reduce.6
  65.3 33.4 all-reduce.8
  122.6 33.4 all-reduce.10
  159.0 34.9 all-reduce.12
  196.2 22.0 all-reduce.14
  221.1 32.7 all-reduce.16
where the time goes:
time: 263 us
  waiting for transfers between devices  206 us (78%)
  matrix products  29.5 us (11%)
  between operations  14.3 us (5%)
  starting transfers between devices  8.29 us (3%)
    psum x4, waiting for transfers between devices, solve_block(): return lax.psum(partial_sum, 'prow')  131 us
    psum x1, waiting for transfers between devices, shards(): across = lax.psum(root_local, 'pcol')  35.1 us
    psum x1, waiting for transfers between devices, shards(): root_update = lax.psum(across, 'grid')  24.1 us
    ppermute x4, waiting for transfers between devices, from_partner(): lax.ppermute(shard, axis, [(i, i ^ 1 << bit) for i in range(lax.axis_size...  15.8 us
    dot_general x6, matrix products, shards(): jnp.dot(kept[source], factor_tile, preferred_element_type=jnp.float32)  14.9 us
    dot_general x4, matrix products, solve_block(): jnp.dot(residual.astype(jnp.bfloat16), inverse, preferred_element_type=jn...  9.38 us
    ppermute x4, starting transfers between devices, from_partner(): lax.ppermute(shard, axis, [(i, i ^ 1 << bit) for i in range(lax.axis_size...  8.05 us
  transfers between devices with their start and end apart: 10, of which 10 were waited for; matrix products, arithmetic and copies ran while one was open for 4% of the time, Pallas kernels for 0%

commit v1 on v0

--- a/solution.py
+++ b/solution.py
@@ -69,7 +69,9 @@
         root_local = root_local + jnp.dot(
             kept[source], factor_tile, preferred_element_type=jnp.float32
         )
-    across = lax.psum(root_local, "pcol")
+    across = root_local
+    for hop in (1, 2):
+        across = across + lax.ppermute(across, "pcol", [(dev, dev ^ hop) for dev in range(4)])
     root_update = lax.psum(across, "grid")
     root_solution = solve_block(root_rhs - root_update, root_inverse)
     return (jnp.stack(solved_all), root_solution)

time: 263 us -> 242 us (0.920)
  waiting for transfers between devices: 206 us -> 182 us
  starting transfers between devices: 8.29 us -> 12.3 us
    psum x1 -> x0, waiting for transfers between devices: 35.1 us -> none  [shards(): across = lax.psum(root_local, 'pcol')]
    ppermute x0 -> x2, waiting for transfers between devices: none -> 11.1 us  [shards(): lax.ppermute(across, 'pcol', [(dev, dev ^ hop) for dev in range(4)])]
    ppermute x0 -> x2, starting transfers between devices: none -> 4.02 us  [shards(): lax.ppermute(across, 'pcol', [(dev, dev ^ hop) for dev in range(4)])]
  transfers between devices with their start and end apart: 10 -> 11, of which waited for: 10 -> 11; matrix products, arithmetic and copies ran while one was open for 4% -> 5% of each run, Pallas kernels for 0% -> 0%
where the time goes in v1:
time: 242 us
  waiting for transfers between devices  182 us (75%)
  matrix products  28.8 us (12%)
  between operations  13.9 us (6%)
  starting transfers between devices  12.3 us (5%)
  other arithmetic  3.17 us (1%)
    psum x4, waiting for transfers between devices, solve_block(): return lax.psum(partial_sum, 'prow')  131 us
    psum x1, waiting for transfers between devices, shards(): root_update = lax.psum(across, 'grid')  24 us
    ppermute x4, waiting for transfers between devices, from_partner(): lax.ppermute(shard, axis, [(i, i ^ 1 << bit) for i in range(lax.axis_size...  15.8 us
    dot_general x6, matrix products, shards(): jnp.dot(kept[source], factor_tile, preferred_element_type=jnp.float32)  14.3 us
    ppermute x2, waiting for transfers between devices, shards(): lax.ppermute(across, 'pcol', [(dev, dev ^ hop) for dev in range(4)])  11.1 us
    dot_general x4, matrix products, solve_block(): jnp.dot(residual.astype(jnp.bfloat16), inverse, preferred_element_type=jn...  9.38 us
    ppermute x4, starting transfers between devices, from_partner(): lax.ppermute(shard, axis, [(i, i ^ 1 << bit) for i in range(lax.axis_size...  8.05 us
    dot_general x6, matrix products, masked(): jnp.dot(row_select, mask.astype(jnp.float32))  5.14 us
  transfers between devices with their start and end apart: 11, of which 11 were waited for; matrix products, arithmetic and copies ran while one was open for 5% of the time, Pallas kernels for 0%

profile of v1, /device:TPU:0, one launch (start us, length us, event | category | flops | bytes accessed | tf_op | source)
XLA Modules:
  0.0 242.0 jit_solution(14567248684123717870)
XLA Ops:
  7.2 2.5 %fusion.22 = f32[64,768]{1,0:T(8,128)} fusion(bf16[3,768,768]{2,1,0:T(8,128)(2,1)} %param.10, f32[1,3,64,768]{3,2,1,0:T(8,128)} %param.8), kind=kOutput, calls=%fused_computation.28 | convolution fusion | flops 75497472 | bytes 1474560 | tf_op jit(solution)/shard_map/dot_general | solution.py:25
  11.1 34.6 %all-reduce.6.cloned.1.call-done = f32[64,768]{1,0:T(8,128)} async-done(((f32[64,768]{1,0:T(8,128)}), f32[64,768]{1,0:T(8,128)}) %all-reduce.6.cloned.1.call-update) | async-done | bytes 196624 | tf_op jit(solution)/shard_map/psum | solution.py:28
  45.7 2.1 fusion.11
  50.3 3.2 %collective-permute-done = f32[64,768]{1,0:T(8,128)S(1)} collective-permute-done((f32[64,768]{1,0:T(8,128)S(1)}, f32[64,768]{1,0:T(8,128)S(1)}, u32[]{:S(2)}, u32[]{:S(2)}) %collective-permute-start) | collective-permute-done | bytes 196640 | tf_op jit(solution)/shard_map/ppermute | solution.py:12
  53.6 2.5 %collective-permute-start.1 = (f32[64,768]{1,0:T(8,128)S(1)}, f32[64,768]{1,0:T(8,128)S(1)}, u32[]{:S(2)}, u32[]{:S(2)}) collective-permute-start(f32[64,768]{1,0:T(8,128)S(1)} %add.64), channel_id=1, source_target_pairs={{0,2},{1,3},{2,0},{3,1},{4,6},{5,7},{6,4},{7,5},{8,10},{9,11},{10,... | collective-permute-start | bytes 589832 | tf_op jit(solution)/shard_map/ppermute | solution.py:12
  57.7 5.2 %collective-permute-done.1 = f32[64,768]{1,0:T(8,128)S(1)} collective-permute-done((f32[64,768]{1,0:T(8,128)S(1)}, f32[64,768]{1,0:T(8,128)S(1)}, u32[]{:S(2)}, u32[]{:S(2)}) %collective-permute-start.1) | collective-permute-done | bytes 196640 | tf_op jit(solution)/shard_map/ppermute | solution.py:12
  62.9 2.3 fusion.19
  66.3 32.6 %all-reduce.8.cloned.1.call-done = f32[64,768]{1,0:T(8,128)} async-done(((f32[64,768]{1,0:T(8,128)}), f32[64,768]{1,0:T(8,128)}) %all-reduce.8.cloned.1.call-update) | async-done | bytes 196624 | tf_op jit(solution)/shard_map/psum | solution.py:28
  98.8 2.8 %fusion.9 = f32[64,768]{1,0:T(8,128)} fusion(bf16[768,24]{1,0:T(8,128)(2,1)S(1)} %fusion.39, bf16[3,768,768]{2,1,0:T(8,128)(2,1)} %param.12, s32[768]{0:T(1024)S(1)} %copy-done.10, f32[64,768]{1,0:T(8,128)} %all-reduce.8.cloned.1.call-done), kind=kOutput, calls=%fused_computation.15 | convolution fusion | flops 104466432 | bytes 1612800 | tf_op jit(solution)/shard_map/dot_general | solution.py:58
  101.7 2.2 fusion.33
  106.4 3.2 %collective-permute-done.2 = f32[64,768]{1,0:T(8,128)S(1)} collective-permute-done((f32[64,768]{1,0:T(8,128)S(1)}, f32[64,768]{1,0:T(8,128)S(1)}, u32[]{:S(2)}, u32[]{:S(2)}) %collective-permute-start.2) | collective-permute-done | bytes 196640 | tf_op jit(solution)/shard_map/ppermute | solution.py:12
  110.6 2.5 %collective-permute-start.3 = (f32[64,768]{1,0:T(8,128)S(1)}, f32[64,768]{1,0:T(8,128)}, u32[]{:S(2)}, u32[]{:S(2)}) collective-permute-start(f32[64,768]{1,0:T(8,128)S(1)} %add.67), channel_id=1, source_target_pairs={{0,2},{1,3},{2,0},{3,1},{4,6},{5,7},{6,4},{7,5},{8,10},{9,11},{10,... | collective-permute-start | bytes 589832 | tf_op jit(solution)/shard_map/ppermute | solution.py:12
  113.0 2.8 %fusion.7 = f32[64,768]{1,0:T(8,128)} fusion(bf16[768,24]{1,0:T(8,128)(2,1)} %fusion.37, bf16[3,768,768]{2,1,0:T(8,128)(2,1)} %param.14, s32[768]{0:T(1024)} %add_select_fusion, f32[64,768]{1,0:T(8,128)S(1)} %copy-done.4), kind=kOutput, calls=%fused_computation.13 | convolution fusion | flops 104466432 | bytes 1773568 | tf_op jit(solution)/shard_map/dot_general | solution.py:69
  115.9 4.1 %collective-permute-done.3 = f32[64,768]{1,0:T(8,128)} collective-permute-done((f32[64,768]{1,0:T(8,128)S(1)}, f32[64,768]{1,0:T(8,128)}, u32[]{:S(2)}, u32[]{:S(2)}) %collective-permute-start.3) | collective-permute-done | bytes 196640 | tf_op jit(solution)/shard_map/ppermute | solution.py:12
  120.0 2.4 fusion.15
  122.5 2.1 fusion.34
  124.6 31.4 %all-reduce.10.cloned.1.call-done = f32[64,768]{1,0:T(8,128)} async-done(((f32[64,768]{1,0:T(8,128)}), f32[64,768]{1,0:T(8,128)}) %all-reduce.10.cloned.1.call-update) | async-done | bytes 196624 | tf_op jit(solution)/shard_map/psum | solution.py:28
  156.0 2.1 fusion.35
  159.8 4.2 %collective-permute-done.4 = f32[64,768]{1,0:T(8,128)S(1)} collective-permute-done((f32[64,768]{1,0:T(8,128)S(1)}, f32[64,768]{1,0:T(8,128)S(1)}, u32[]{:S(2)}, u32[]{:S(2)}) %collective-permute-start.4) | collective-permute-done | bytes 196640 | tf_op jit(solution)/shard_map/ppermute | solution.py:74
  164.0 2.5 %collective-permute-start.5 = (f32[64,768]{1,0:T(8,128)S(1)}, f32[64,768]{1,0:T(8,128)S(1)}, u32[]{:S(2)}, u32[]{:S(2)}) collective-permute-start(f32[64,768]{1,0:T(8,128)S(1)} %add.71), channel_id=1, source_target_pairs={{0,2},{1,3},{2,0},{3,1},{4,6},{5,7},{6,4},{7,5},{8,10},{9,11},{10,... | collective-permute-start | bytes 589832 | tf_op jit(solution)/shard_map/ppermute | solution.py:74
  166.4 6.9 %collective-permute-done.5 = f32[64,768]{1,0:T(8,128)S(1)} collective-permute-done((f32[64,768]{1,0:T(8,128)S(1)}, f32[64,768]{1,0:T(8,128)S(1)}, u32[]{:S(2)}, u32[]{:S(2)}) %collective-permute-start.5) | collective-permute-done | bytes 196640 | tf_op jit(solution)/shard_map/ppermute | solution.py:74
  174.1 24.0 %all-reduce.12.cloned.1.call-done = f32[64,768]{1,0:T(8,128)} async-done(((f32[64,768]{1,0:T(8,128)}), f32[64,768]{1,0:T(8,128)}) %all-reduce.12.cloned.1.call-update) | async-done | bytes 196624 | tf_op jit(solution)/shard_map/psum | solution.py:75
  198.1 2.2 fusion.62
  201.2 32.5 %all-reduce.14.cloned.1.call-done = f32[64,1536]{1,0:T(8,128)} async-done(((f32[64,1536]{1,0:T(8,128)}), f32[64,1536]{1,0:T(8,128)}) %all-reduce.14.cloned.1.call-update) | async-done | bytes 393232 | tf_op jit(solution)/shard_map/psum | solution.py:28
  (51 shorter events, 15.1 us)
Async XLA Ops:
  7.2 190.9 %copy-start = (bf16[768,1536]{1,0:T(8,128)(2,1)S(1)}, bf16[768,1536]{1,0:T(8,128)(2,1)}, u32[]{:S(2)}) copy-start(bf16[768,1536]{1,0:T(8,128)(2,1)} %param.11) | copy-start | bytes 7077892
  7.2 2.7 %copy-start.8 = (s32[3,6,24]{2,1,0:T(8,128)S(1)}, s32[3,6,24]{2,1,0:T(8,128)}, u32[]{:S(2)}) copy-start(s32[3,6,24]{2,1,0:T(8,128)} %param.13) | copy-start | bytes 5188
  7.2 38.5 %all-reduce.6.cloned.1.call-start = ((), (), s32[]{:S(2)}) async-start(), calls=%async_computation | async-start | bytes 393216 | tf_op jit(solution)/shard_map/psum | solution.py:28
  9.8 89.0 %all-reduce.8.cloned.1.call-start = ((), (), s32[]{:S(2)}) async-start(), calls=%async_computation.1 | async-start | bytes 393216 | tf_op jit(solution)/shard_map/psum | solution.py:28
  11.0 51.9 %copy-start.1 = (f32[1,3,64,768]{3,2,1,0:T(8,128)S(1)}, f32[1,3,64,768]{3,2,1,0:T(8,128)}, u32[]{:S(2)}) copy-start(f32[1,3,64,768]{3,2,1,0:T(8,128)} %param.8) | copy-start | bytes 1769476
  47.8 5.7 %collective-permute-start = (f32[64,768]{1,0:T(8,128)S(1)}, f32[64,768]{1,0:T(8,128)S(1)}, u32[]{:S(2)}, u32[]{:S(2)}) collective-permute-start(f32[64,768]{1,0:T(8,128)S(1)} %fusion.11), channel_id=1, source_target_pairs={{0,1},{1,0},{2,3},{3,2},{4,5},{5,4},{6,7},{7,6},{8,9},{9,8},{10,11... | collective-permute-start | bytes 589832 | tf_op jit(solution)/shard_map/ppermute | solution.py:12
  53.6 11.7 %copy-start.9 = (s32[3,6,24]{2,1,0:T(8,128)S(1)}, s32[3,6,24]{2,1,0:T(8,128)}, u32[]{:S(2)}) copy-start(s32[3,6,24]{2,1,0:T(8,128)} %param.15) | copy-start | bytes 5188
  53.6 9.4 %collective-permute-start.1 = (f32[64,768]{1,0:T(8,128)S(1)}, f32[64,768]{1,0:T(8,128)S(1)}, u32[]{:S(2)}, u32[]{:S(2)}) collective-permute-start(f32[64,768]{1,0:T(8,128)S(1)} %add.64), channel_id=1, source_target_pairs={{0,2},{1,3},{2,0},{3,1},{4,6},{5,7},{6,4},{7,5},{8,10},{9,11},{10,... | collective-permute-start | bytes 589832 | tf_op jit(solution)/shard_map/ppermute | solution.py:12
  57.7 41.1 %copy-start.10 = (s32[768]{0:T(1024)S(1)}, s32[768]{0:T(1024)}, u32[]{:S(2)}) copy-start(s32[768]{0:T(1024)} %add_select_fusion) | copy-start | bytes 9220
  65.2 36.4 %copy-start.3 = (f32[64,768]{1,0:T(8,128)S(1)}, f32[64,768]{1,0:T(8,128)}, u32[]{:S(2)}) copy-start(f32[64,768]{1,0:T(8,128)} %all-reduce.6.cloned.1.call-done) | copy-start | bytes 589828
  65.2 90.8 %all-reduce.10.cloned.1.call-start = ((), (), s32[]{:S(2)}) async-start(), calls=%async_computation.2 | async-start | bytes 393216 | tf_op jit(solution)/shard_map/psum | solution.py:28
  101.7 11.4 %copy-start.4 = (f32[64,768]{1,0:T(8,128)S(1)}, f32[64,768]{1,0:T(8,128)}, u32[]{:S(2)}) copy-start(f32[64,768]{1,0:T(8,128)} %all-reduce.8.cloned.1.call-done) | copy-start | bytes 589828
  103.9 2.5 %copy-start.7 = (f32[64,768]{1,0:T(8,128)}, f32[64,768]{1,0:T(8,128)S(1)}, u32[]{:S(2)}) copy-start(f32[64,768]{1,0:T(8,128)S(1)} %fusion.33) | copy-start | bytes 589828
  103.9 5.7 %collective-permute-start.2 = (f32[64,768]{1,0:T(8,128)S(1)}, f32[64,768]{1,0:T(8,128)S(1)}, u32[]{:S(2)}, u32[]{:S(2)}) collective-permute-start(f32[64,768]{1,0:T(8,128)S(1)} %fusion.33), channel_id=1, source_target_pairs={{0,1},{1,0},{2,3},{3,2},{4,5},{5,4},{6,7},{7,6},{8,9},{9,8},{10,11... | collective-permute-start | bytes 589832 | tf_op jit(solution)/shard_map/ppermute | solution.py:12
  110.6 9.5 %collective-permute-start.3 = (f32[64,768]{1,0:T(8,128)S(1)}, f32[64,768]{1,0:T(8,128)}, u32[]{:S(2)}, u32[]{:S(2)}) collective-permute-start(f32[64,768]{1,0:T(8,128)S(1)} %add.67), channel_id=1, source_target_pairs={{0,2},{1,3},{2,0},{3,1},{4,6},{5,7},{6,4},{7,5},{8,10},{9,11},{10,... | collective-permute-start | bytes 589832 | tf_op jit(solution)/shard_map/ppermute | solution.py:12
  115.9 6.6 %copy-start.11 = (s32[768]{0:T(1024)S(1)}, s32[768]{0:T(1024)}, u32[]{:S(2)}) copy-start(s32[768]{0:T(1024)} %add_select_fusion) | copy-start | bytes 9220
  122.4 33.6 %copy-start.6 = (bf16[768,24]{1,0:T(8,128)(2,1)S(1)}, bf16[768,24]{1,0:T(8,128)(2,1)}, u32[]{:S(2)}) copy-start(bf16[768,24]{1,0:T(8,128)(2,1)} %fusion.36) | copy-start | bytes 110596
  122.4 75.6 %all-reduce.12.cloned.1.call-start = ((), (), s32[]{:S(2)}) async-start(), calls=%async_computation.3 | async-start | bytes 393216 | tf_op jit(solution)/shard_map/psum | solution.py:75
  158.2 39.9 %copy-start.2 = (f32[64,768]{1,0:T(8,128)S(1)}, f32[64,768]{1,0:T(8,128)}, u32[]{:S(2)}) copy-start(f32[64,768]{1,0:T(8,128)} %param.9) | copy-start | bytes 589828
  158.2 5.7 %collective-permute-start.4 = (f32[64,768]{1,0:T(8,128)S(1)}, f32[64,768]{1,0:T(8,128)S(1)}, u32[]{:S(2)}, u32[]{:S(2)}) collective-permute-start(f32[64,768]{1,0:T(8,128)S(1)} %fusion.35), channel_id=1, source_target_pairs={{0,1},{1,0},{2,3},{3,2},{4,5},{5,4},{6,7},{7,6},{8,9},{9,8},{10,11... | collective-permute-start | bytes 589832 | tf_op jit(solution)/shard_map/ppermute | solution.py:74
  164.0 9.3 %collective-permute-start.5 = (f32[64,768]{1,0:T(8,128)S(1)}, f32[64,768]{1,0:T(8,128)S(1)}, u32[]{:S(2)}, u32[]{:S(2)}) collective-permute-start(f32[64,768]{1,0:T(8,128)S(1)} %add.71), channel_id=1, source_target_pairs={{0,2},{1,3},{2,0},{3,1},{4,6},{5,7},{6,4},{7,5},{8,10},{9,11},{10,... | collective-permute-start | bytes 589832 | tf_op jit(solution)/shard_map/ppermute | solution.py:74
  174.0 26.2 %copy-start.5 = (f32[64,768]{1,0:T(8,128)S(1)}, f32[64,768]{1,0:T(8,128)}, u32[]{:S(2)}) copy-start(f32[64,768]{1,0:T(8,128)} %all-reduce.10.cloned.1.call-done) | copy-start | bytes 589828
  174.1 59.6 %all-reduce.14.cloned.1.call-start = ((), (), s32[]{:S(2)}) async-start(), calls=%async_computation.4 | async-start | bytes 786432 | tf_op jit(solution)/shard_map/psum | solution.py:28
Sparse Core Ops, SparseCore 0:
  10.9 34.7 all-reduce.5
  65.3 33.4 all-reduce.7
  122.6 33.4 all-reduce.9
  174.2 23.8 all-reduce.11
  200.8 32.7 all-reduce.13
